TPU v7x, 8 devices: a whole 2x2x1 slice. The times are simulated.
8 devices in a mesh: dp: 1 (over z), sp: 8 (over y, x, core).
Axes of the slice: x: 2, y: 2, z: 1, core: 2. Of those that a mesh axis runs over, the one named last changes fastest.
Arguments:
- tokens: bfloat16 [16384, 768], P(('dp', 'sp'))
- grad_out: bfloat16 [16384, 768], P(('dp', 'sp'))
- ln_gain: float32 [768], replicated
- ln_bias: float32 [768], replicated
- w_qkv: bfloat16 [768, 2304], replicated
- w_out: bfloat16 [768, 768], replicated
- temperature: float32 [16], replicated
Outputs:
- output 1: bfloat16 [16384, 768], P(('dp', 'sp'))
- output 2: bfloat16 [16384, 768], P(('dp', 'sp'))
- output 3: float32 [768, 2304], P(('dp', 'sp'))
- output 4: float32 [768, 768], P(('dp', 'sp'))
- output 5: float32 [768], P('dp')
- output 6: float32 [768], P('dp')
- output 7: float32 [16], P('dp')
All inputs are finite; a program needn't handle non-finite values.
Results may differ from a plain program's by a relative error of at most 0.0014325.
Values are sent between devices in bfloat16 or wider.
A program may use at most 1 GiB of HBM per device.

v0:
```python
import jax
import jax.numpy as jnp
from jax import lax
from jax.experimental import pallas as pl
from jax.experimental.pallas import tpu as pltpu
from jax.sharding import PartitionSpec as P

F32 = jnp.float32
BF16 = jnp.bfloat16
MESH = pl.DeviceIdType.MESH

ROWS = 2048
WIDTH = 768
HEADS = 16
HD = 48
GW = 384
GH = 8
BLK = 512
NBLK = ROWS // BLK
LNR = 32
PAY = 400
HALF = PAY // 2
SHARD = 96
CHUNKS = 8


def dot(a, b, ca, cb):
    return lax.dot_general(a, b, (((ca,), (cb,)), ((), ())), preferred_element_type=F32)


def kernel(temp_ref, gain_ref, bias_ref, x_hbm, dy_hbm, wqkv_hbm, wout_hbm,
           out_hbm, gtok_hbm, gwqkv_hbm, gwout_hbm, gb_out, dtemp_out,
           x_v, dy_v, u_v, ut_v, qkv_v, do_v, ot_v, w_v, wo_v,
           gm_v, sq_v, bd_v, dsq_v, row_v, pay_v, ar1, ar2, ar3, sum_v,
           gw_v, r1, r2, r3, fin_v, du_v, gb_v, gbs_v, gbr_v,
           in_sem, w_sem, out_sem, fin_sem,
           ar_send, ar_recv, s1_send, s1_recv, s2_send, s2_recv, s3_send, s3_recv, gb_send, gb_recv):
    dp = lax.axis_index('dp')
    me = lax.axis_index('sp')
    core = me % 2
    cx = (me // 2) % 2
    cy = me // 4
    partner = me + 1 - 2 * core
    xn = me + 2 - 4 * cx
    yn = me + 4 - 8 * cy
    first = xn + core * (yn - xn)
    second = yn + core * (xn - yn)
    ca = cx + core * (cy - cx)
    cb = cy + core * (cx - cy)

    def chip(a, b):
        return a * (1 + core) + b * (2 - core)

    def dev(i):
        return (dp, i)

    def remote(src, dst, ss, rs, to):
        return pltpu.make_async_remote_copy(src_ref=src, dst_ref=dst, send_sem=ss, recv_sem=rs,
                                            device_id=dev(to), device_id_type=MESH)

    barrier = pltpu.get_barrier_semaphore()
    for peer in (partner, xn, yn):
        pl.semaphore_signal(barrier, inc=1, device_id=dev(peer), device_id_type=MESH)

    def w_copy(g, p):
        return pltpu.make_async_copy(wqkv_hbm.at[:, pl.ds(p * WIDTH + g * GW, GW)],
                                     w_v.at[g, :, pl.ds(p * GW, GW)], w_sem.at[3 * g + p])

    wo_copy = pltpu.make_async_copy(wout_hbm, wo_v, w_sem.at[6])

    def x_copy(b):
        rows = pl.ds(b * BLK, BLK)
        return pltpu.make_async_copy(x_hbm.at[rows], x_v.at[rows], in_sem.at[0, b])

    def dy_copy(b):
        rows = pl.ds(b * BLK, BLK)
        return pltpu.make_async_copy(dy_hbm.at[rows], dy_v.at[rows], in_sem.at[1, b])

    x_copy(0).start()
    for p in range(3):
        w_copy(0, p).start()
    dy_copy(0).start()
    wo_copy.start()
    for b in range(1, NBLK):
        x_copy(b).start()
        dy_copy(b).start()
    for p in range(3):
        w_copy(1, p).start()

    gain = gain_ref[...]
    bias = bias_ref[...]

    def normed_rows(r0):
        xf = x_v[pl.ds(r0, LNR), :].astype(F32)
        c = xf - jnp.mean(xf, axis=-1, keepdims=True)
        rstd = lax.rsqrt(jnp.mean(c * c, axis=-1, keepdims=True) + 1e-6)
        return c * rstd, rstd

    def sumsq(v):
        vf = v.astype(F32)
        return jnp.sum((vf * vf).reshape(BLK // 8, 8, GW), axis=0)

    def project(g, b, with_ln):
        r0 = pl.multiple_of(b * BLK, BLK)
        rows = pl.ds(r0, BLK)
        if with_ln:
            for i in range(BLK // LNR):
                xhat, _ = normed_rows(r0 + i * LNR)
                u_v[pl.ds(r0 + i * LNR, LNR), :] = (xhat * gain + bias).astype(BF16)
        u = u_v[rows, :]
        if with_ln:
            ut_v[:, rows] = u.T
            do_v[rows, :] = dot(dy_v[rows, :], wo_v[...], 1, 1).astype(BF16)
        qkv = dot(u, w_v[g], 1, 0).astype(BF16)
        qkv_v[g, rows, :] = qkv
        sq_v[g, 0] += sumsq(qkv[:, :GW])
        sq_v[g, 1] += sumsq(qkv[:, GW:2 * GW])

    def grams(g):
        gm_v[0] = dot(qkv_v[g, :, :GW], qkv_v[g, :, GW:2 * GW], 0, 0)
        gm_v[1] = dot(do_v[:, g * GW:(g + 1) * GW], qkv_v[g, :, 2 * GW:], 0, 0)
        lane = lax.broadcasted_iota(jnp.int32, (HD, 128), 1)
        pay = pay_v.at[g]
        for h in range(GH):
            lo = HD * h // 128 * 128
            hi = min(lo + 256, GW)
            off = HD * h - lo
            a = gm_v[0, HD * h:HD * (h + 1), lo:hi]
            d = gm_v[1, HD * h:HD * (h + 1), lo:hi]
            n = hi - lo
            if off:
                a = pltpu.roll(a, n - off, 1)
            a = a[:, :128]
            s = (64 - off) % n
            if s:
                d = pltpu.roll(d, s, 1)
            d = d[:, :128]
            both = jnp.where(lane < HD, a, jnp.where((lane >= 64) & (lane < 64 + HD), d, 0.0))
            pay[HD * h:HD * (h + 1), :] = both
        pay[GW:PAY, :] = jnp.zeros((PAY - GW, 128), F32)
        for p in range(2):
            row = jnp.sum(sq_v[g, p], axis=0, keepdims=True)
            for c in range(3):
                r = GW + 3 * p + c
                pay[r:r + 1, :] = row[:, 128 * c:128 * (c + 1)]

    mine = pl.ds(pl.multiple_of(core * HALF, 8), HALF)
    theirs = pl.ds(pl.multiple_of((1 - core) * HALF, 8), HALF)

    held = {}

    def ar_step(g, k):
        if k == 1:
            held[g, 0].wait()
            pay_v[g, mine, :] = ar1[g] + pay_v[g, mine, :]
        elif k == 2:
            held[g, 1].wait()
            pay_v[g, mine, :] = ar2[g] + pay_v[g, mine, :]
        elif k == 3:
            held[g, 2].wait()
            sum_v[g, mine, :] = ar3[g] + pay_v[g, mine, :]
        elif k == 4:
            held[g, 3].wait()
            return
        if k == 0:
            src, dst, to = pay_v.at[g, theirs], ar1.at[g], partner
        elif k == 1:
            src, dst, to = pay_v.at[g, mine], ar2.at[g], first
        elif k == 2:
            src, dst, to = pay_v.at[g, mine], ar3.at[g], second
        else:
            src, dst, to = sum_v.at[g, mine], sum_v.at[g, mine], partner
        held[g, k] = remote(src, dst, ar_send.at[g, k], ar_recv.at[g, k], to)
        held[g, k].start()

    def spread(rows3, h):
        wide = jnp.broadcast_to(rows3, (8, GW))
        if h:
            wide = pltpu.roll(wide, GW - HD * h, 1)
        return wide[:1, :128]

    def place(v, h):
        wide = jnp.concatenate([v, jnp.zeros((v.shape[0], GW - 128), v.dtype)], axis=1)
        return pltpu.roll(wide, HD * h, 1) if h else wide

    def small(g):
        sqrow = jnp.concatenate([sum_v[g, GW + c:GW + c + 1, :] for c in range(3)], axis=1)
        skrow = jnp.concatenate([sum_v[g, GW + 3 + c:GW + 4 + c, :] for c in range(3)], axis=1)
        for c in range(3):
            row_v[128 * c:128 * (c + 1), :] = jnp.broadcast_to(sqrow[:, 128 * c:128 * (c + 1)], (128, 128)).T
        lane = lax.broadcasted_iota(jnp.int32, (HD, 128), 1)
        ok = lane < HD
        dsk = jnp.zeros((8, GW), F32)
        for h in range(GH):
            hr = slice(HD * h, HD * (h + 1))
            both = sum_v[g, hr, :]
            gram = jnp.where(ok, both, 0.0)
            da = jnp.where(ok, pltpu.roll(both, 64, 1), 0.0)
            sqc = row_v[hr, :]
            skh = jnp.broadcast_to(spread(skrow, h), (HD, 128))
            skh = jnp.where(ok, skh, 1.0)
            den = jnp.sqrt(sqc) * jnp.sqrt(skh)
            cosine = gram / den
            t = temp_ref[g * GH + h]
            logit = jnp.where(ok, t * cosine, -jnp.inf)
            top = jnp.max(logit, axis=1, keepdims=True)
            e = jnp.where(ok, jnp.exp(logit - top), 0.0)
            a = e / jnp.sum(e, axis=1, keepdims=True)
            ds = a * (da - jnp.sum(a * da, axis=1, keepdims=True))
            dtemp_out[g * GH + h:g * GH + h + 1, :] = jnp.broadcast_to(
                jnp.sum(jnp.sum(ds * cosine, axis=1, keepdims=True), axis=0, keepdims=True), (1, 128))
            dcos = t * ds
            dg = dcos / den
            w = dcos * cosine
            row_v[hr, :] = -jnp.sum(w, axis=1, keepdims=True) / sqc
            dskh = jnp.sum(w, axis=0, keepdims=True) / skh[:1]
            dsk = dsk + place(jnp.broadcast_to(-dskh, (8, 128)), h)
            bd_v[g, 0, hr, :] = place(a, h).astype(BF16)
            bd_v[g, 1, hr, :] = place(dg, h).astype(BF16)
        dsq_v[g, 8:16, :] = dsk
        dsq_v[g, 0:8, :] = jnp.concatenate(
            [row_v[128 * c:128 * (c + 1), :].T[:8] for c in range(3)], axis=1)

    def heads(g, b):
        rows = pl.ds(pl.multiple_of(b * BLK, BLK), BLK)
        cols = slice(g * GW, (g + 1) * GW)
        attn = bd_v[g, 0]
        dgram = bd_v[g, 1]
        dsq = dsq_v[g, 0:1, :]
        dsk = dsq_v[g, 8:9, :]
        q = qkv_v[g, rows, :GW]
        k = qkv_v[g, rows, GW:2 * GW]
        v = qkv_v[g, rows, 2 * GW:]
        do = do_v[rows, cols]
        o = dot(v, attn, 1, 1).astype(BF16)
        dq = (dot(k, dgram, 1, 1) + q.astype(F32) * dsq).astype(BF16)
        dk = (dot(q, dgram, 1, 0) + k.astype(F32) * dsk).astype(BF16)
        dv = dot(do, attn, 1, 0).astype(BF16)
        qkv_v[g, rows, :GW] = dq
        qkv_v[g, rows, GW:2 * GW] = dk
        qkv_v[g, rows, 2 * GW:] = dv
        do_v[rows, cols] = o
        ot_v[cols, rows] = o.T

    def gw_chunk(ch):
        def half(m, carry):
            mr = pl.ds(pl.multiple_of(m * GW, GW), GW)
            if ch < 6:
                g, p = divmod(ch, 3)
                res = dot(ut_v[mr, :], qkv_v[g, :, p * GW:(p + 1) * GW], 1, 0)
            else:
                res = dot(ot_v[mr, :], dy_v[:, (ch - 6) * GW:(ch - 5) * GW], 1, 0)
            gw_v[ch, pl.ds(2 * m, 2)] = res.reshape(2, 2, SHARD, GW)
            return carry
        lax.fori_loop(0, 2, half, 0)

    def s1(ch):
        c = remote(gw_v.at[ch, :, 1 - core], r1.at[ch], s1_send.at[ch], s1_recv.at[ch], partner)
        c.start()
        held['s1', ch] = c

    def s2(ch):
        held['s1', ch].wait()
        for a, b in ((1 - ca, 1 - cb), (1 - ca, cb), (ca, 1 - cb), (ca, cb)):
            i = chip(a, b)
            r1[ch, i] += gw_v[ch, i, core]
        for n, b in ((0, 1 - cb), (1, cb)):
            c = remote(r1.at[ch, chip(1 - ca, b)], r2.at[ch, b], s2_send.at[ch, b], s2_recv.at[ch, b], first)
            c.start()
            held['s2', ch, n] = c

    def s3(ch):
        held['s2', ch, 0].wait()
        held['s2', ch, 1].wait()
        for b in (1 - cb, cb):
            r2[ch, b] += r1[ch, chip(ca, b)]
        c = remote(r2.at[ch, 1 - cb], r3.at[ch], s3_send.at[ch], s3_recv.at[ch], second)
        c.start()
        held['s3', ch] = c

    def s4(ch):
        held['s3', ch].wait()
        fin_v[ch] = r3[ch] + r2[ch, cb]
        if ch < 6:
            g, p = divmod(ch, 3)
            dst = gwqkv_hbm.at[:, pl.ds(p * WIDTH + g * GW, GW)]
        else:
            dst = gwout_hbm.at[:, pl.ds((ch - 6) * GW, GW)]
        c = pltpu.make_async_copy(fin_v.at[ch], dst, fin_sem.at[ch])
        c.start()
        held['fin', ch] = c

    gsum = (jnp.zeros((8, WIDTH), F32), jnp.zeros((8, WIDTH), F32))

    def final_block(b):
        r0 = pl.multiple_of(b * BLK, BLK)
        rows = pl.ds(r0, BLK)
        du_v[...] = dot(qkv_v[0, rows, :], w_v[0], 1, 1) + dot(qkv_v[1, rows, :], w_v[1], 1, 1)
        do_v[rows, :] = (x_v[rows, :].astype(F32) + dot(do_v[rows, :], wo_v[...], 1, 0)).astype(BF16)
        pltpu.make_async_copy(do_v.at[rows], out_hbm.at[rows], out_sem.at[0, b]).start()
        dgain = jnp.zeros((8, WIDTH), F32)
        dbias = jnp.zeros((8, WIDTH), F32)
        for i in range(BLK // LNR):
            sub = pl.ds(r0 + i * LNR, LNR)
            xhat, rstd = normed_rows(r0 + i * LNR)
            du = du_v[i * LNR:(i + 1) * LNR, :]
            dgain = dgain + jnp.sum((du * xhat).reshape(LNR // 8, 8, WIDTH), axis=0)
            dbias = dbias + jnp.sum(du.reshape(LNR // 8, 8, WIDTH), axis=0)
            dxh = du * gain
            m1 = jnp.mean(dxh, axis=-1, keepdims=True)
            m2 = jnp.mean(dxh * xhat, axis=-1, keepdims=True)
            dx = rstd * (dxh - m1 - xhat * m2)
            x_v[sub, :] = (dy_v[sub, :].astype(F32) + dx).astype(BF16)
        gb_v[0] += dgain
        gb_v[1] += dbias
        pltpu.make_async_copy(x_v.at[rows], gtok_hbm.at[rows], out_sem.at[1, b]).start()

    def gb_start(k):
        to = (partner, first, second)[k]
        c = remote(gbs_v.at[k], gbr_v.at[k], gb_send.at[k], gb_recv.at[k], to)
        c.start()
        held['gb', k] = c

    def gb_next(k):
        held['gb', k].wait()
        total = gbs_v[k] + gbr_v[k]
        if k < 2:
            gbs_v[k + 1] = total
            gb_start(k + 1)
        else:
            gb_out[...] = total

    sq_v[...] = jnp.zeros_like(sq_v)
    gb_v[...] = jnp.zeros_like(gb_v)
    for p in range(3):
        w_copy(0, p).wait()
    wo_copy.wait()

    def first_pass(b, carry):
        x_copy(b).wait()
        dy_copy(b).wait()
        project(0, b, True)
        return carry
    lax.fori_loop(0, NBLK, first_pass, 0)
    grams(0)
    pl.semaphore_wait(barrier, 3)
    ar_step(0, 0)
    for p in range(3):
        w_copy(1, p).wait()

    def loop(f, lo, hi):
        def body(b, carry):
            f(b)
            return carry
        lax.fori_loop(lo, hi, body, 0)

    loop(lambda b: project(1, b, False), 0, 1)
    ar_step(0, 1)
    loop(lambda b: project(1, b, False), 1, 3)
    ar_step(0, 2)
    loop(lambda b: project(1, b, False), 3, 4)
    grams(1)
    ar_step(1, 0)
    ar_step(0, 3)
    ar_step(1, 1)
    ar_step(0, 4)
    small(0)
    ar_step(1, 2)
    loop(lambda b: heads(0, b), 0, NBLK)
    ar_step(1, 3)
    gw_chunk(0)
    s1(0)
    gw_chunk(1)
    s1(1)
    s2(0)
    gw_chunk(2)
    s1(2)
    s2(1)
    ar_step(1, 4)
    small(1)
    s2(2)
    loop(lambda b: heads(1, b), 0, NBLK)
    s3(0)
    gw_chunk(3)
    s1(3)
    s3(1)
    gw_chunk(4)
    s1(4)
    s2(3)
    gw_chunk(5)
    s1(5)
    s2(4)
    s3(2)
    gw_chunk(6)
    s1(6)
    s2(5)
    gw_chunk(7)
    s1(7)
    s2(6)
    s3(3)
    final_block(0)
    s2(7)
    s3(4)
    final_block(1)
    s3(5)
    final_block(2)
    s3(6)
    final_block(3)
    gbs_v[0] = jnp.concatenate([jnp.sum(gb_v[i], axis=0, keepdims=True) for i in range(2)]
                               + [jnp.zeros((6, WIDTH), F32)], axis=0)
    gb_start(0)
    for ch in range(0, 4):
        s4(ch)
    gb_next(0)
    for ch in range(4, 6):
        s4(ch)
    s3(7)
    gb_next(1)
    s4(6)
    gb_next(2)
    s4(7)
    for b in range(NBLK):
        rows = pl.ds(b * BLK, BLK)
        pltpu.make_async_copy(do_v.at[rows], out_hbm.at[rows], out_sem.at[0, b]).wait()
        pltpu.make_async_copy(x_v.at[rows], gtok_hbm.at[rows], out_sem.at[1, b]).wait()
    for ch in range(CHUNKS):
        held['fin', ch].wait()


def block_step(x, dy, ln_gain, ln_bias, w_qkv, w_out, temperature):
    any_spec = pl.BlockSpec(memory_space=pl.ANY)
    vmem = pl.BlockSpec(memory_space=pltpu.VMEM)
    dma = pltpu.SemaphoreType.DMA
    return pl.pallas_call(
        kernel,
        out_shape=(
            jax.ShapeDtypeStruct((ROWS, WIDTH), BF16),
            jax.ShapeDtypeStruct((ROWS, WIDTH), BF16),
            jax.ShapeDtypeStruct((SHARD, 3 * WIDTH), F32),
            jax.ShapeDtypeStruct((SHARD, WIDTH), F32),
            jax.ShapeDtypeStruct((8, WIDTH), F32),
            jax.ShapeDtypeStruct((HEADS, 128), F32),
        ),
        in_specs=[pl.BlockSpec(memory_space=pltpu.SMEM), vmem, vmem, any_spec, any_spec, any_spec, any_spec],
        out_specs=(any_spec, any_spec, any_spec, any_spec, vmem, vmem),
        scratch_shapes=[
            pltpu.VMEM((ROWS, WIDTH), BF16),
            pltpu.VMEM((ROWS, WIDTH), BF16),
            pltpu.VMEM((ROWS, WIDTH), BF16),
            pltpu.VMEM((WIDTH, ROWS), BF16),
            pltpu.VMEM((2, ROWS, 3 * GW), BF16),
            pltpu.VMEM((ROWS, WIDTH), BF16),
            pltpu.VMEM((WIDTH, ROWS), BF16),
            pltpu.VMEM((2, WIDTH, 3 * GW), BF16),
            pltpu.VMEM((WIDTH, WIDTH), BF16),
            pltpu.VMEM((2, GW, GW), F32),
            pltpu.VMEM((2, 2, 8, GW), F32),
            pltpu.VMEM((2, 2, GW, GW), BF16),
            pltpu.VMEM((2, 16, GW), F32),
            pltpu.VMEM((GW, 128), F32),
            pltpu.VMEM((2, PAY, 128), F32),
            pltpu.VMEM((2, HALF, 128), F32),
            pltpu.VMEM((2, HALF, 128), F32),
            pltpu.VMEM((2, HALF, 128), F32),
            pltpu.VMEM((2, PAY, 128), F32),
            pltpu.VMEM((CHUNKS, 4, 2, SHARD, GW), F32),
            pltpu.VMEM((CHUNKS, 4, SHARD, GW), F32),
            pltpu.VMEM((CHUNKS, 2, SHARD, GW), F32),
            pltpu.VMEM((CHUNKS, SHARD, GW), F32),
            pltpu.VMEM((CHUNKS, SHARD, GW), F32),
            pltpu.VMEM((BLK, WIDTH), F32),
            pltpu.VMEM((2, 8, WIDTH), F32),
            pltpu.VMEM((3, 8, WIDTH), F32),
            pltpu.VMEM((3, 8, WIDTH), F32),
            dma((2, NBLK)), dma((7,)), dma((2, NBLK)), dma((CHUNKS,)),
            dma((2, 4)), dma((2, 4)),
            dma((CHUNKS,)), dma((CHUNKS,)),
            dma((CHUNKS, 2)), dma((CHUNKS, 2)),
            dma((CHUNKS,)), dma((CHUNKS,)),
            dma((3,)), dma((3,)),
        ],
        compiler_params=pltpu.CompilerParams(
            collective_id=0, has_side_effects=True, vmem_limit_bytes=67043328),
    )(temperature, ln_gain.reshape(1, WIDTH), ln_bias.reshape(1, WIDTH), x, dy, w_qkv, w_out)


def solution(mesh):
    row_spec = P(('dp', 'sp'), None)
    part_spec = P('dp')
    full_spec = P()

    def local_step(x, dy, ln_gain, ln_bias, w_qkv, w_out, temperature):
        out, gtok, gwqkv, gwout, gb, dtemp = block_step(x, dy, ln_gain, ln_bias, w_qkv, w_out, temperature)
        return out, gtok, gwqkv, gwout, gb[0], gb[1], dtemp[:, 0]

    return jax.shard_map(local_step, mesh=mesh,
                         in_specs=(row_spec, row_spec, full_spec, full_spec, full_spec, full_spec, full_spec),
                         out_specs=(row_spec, row_spec, row_spec, row_spec, part_spec, part_spec, part_spec),
                         check_vma=False)
```

profile of v0, /device:TPU:0, one launch (start us, length us, event | category | flops | bytes accessed | tf_op | source)
XLA Modules:
  0.0 98.1 jit_solution(8224054902691943624)
XLA Ops:
  0.6 1.3 %reshape.20.gain_ref = f32[1,768]{1,0:T(1,128)} reshape(f32[768]{0:T(1024)} %param.9) | data formatting | bytes 6144 | tf_op jit(solution)/shard_map/reshape | solution.py:484
  1.9 1.3 %reshape.21.bias_ref = f32[1,768]{1,0:T(1,128)} reshape(f32[768]{0:T(1024)} %param.10) | data formatting | bytes 6144 | tf_op jit(solution)/shard_map/reshape | solution.py:484
  3.2 84.8 %shard_map.126 = (bf16[2048,768]{1,0:T(8,128)(2,1)}, bf16[2048,768]{1,0:T(8,128)(2,1)}, f32[96,2304]{1,0:T(8,128)}, f32[96,768]{1,0:T(8,128)}, f32[8,768]{1,0:T(8,128)}, /*index=5*/f32[16,128]{1,0:T(8,128)}) custom-call(f32[16]{0:T(128)} %temp_ref.1, f32[1,768]{1,0:T(1,128)} %reshape.20.gain_ref, f32[1,768]{1,0:T(1,128)} %reshape.21.bias_ref, ...), custom_call_target="tpu_custom_call" | custom-call | tf_op jit(solution)/shard_map/pallas_call | solution.py:434
  88.0 1.4 %slice_reduce_fusion.1 = (f32[768]{0:T(1024)}, f32[768]{0:T(1024)}) fusion(f32[8,768]{1,0:T(8,128)} %get-tuple-element.17), kind=kLoop, calls=%fused_computation.1 | loop fusion | bytes 12288 | tf_op jit(solution)/shard_map/slice | solution.py:494
  89.4 1.3 %slice_reduce_fusion = f32[16]{0:T(128)} fusion(f32[16,128]{1,0:T(8,128)} %get-tuple-element.18), kind=kLoop, calls=%fused_computation | loop fusion | bytes 128 | tf_op jit(solution)/shard_map/slice | solution.py:494
  90.7 0.0 copy-start
  90.7 3.9 %copy.18 = bf16[2048,768]{1,0:T(8,128)(2,1)} copy(bf16[2048,768]{1,0:T(8,128)(2,1)} %get-tuple-element.28) | data formatting | bytes 6291456
  94.6 0.0 copy-done
  94.7 0.0 copy-start.1
  94.7 0.0 copy-start.2
  94.7 1.7 %copy.19 = bf16[2048,768]{1,0:T(8,128)(2,1)} copy(bf16[2048,768]{1,0:T(8,128)(2,1)S(1)} %copy-done) | data formatting | bytes 6291456
  96.3 0.1 copy-done.1
  96.4 0.9 copy.20
  97.3 0.0 copy-done.2
  97.3 0.7 copy.21
Async XLA Ops:
  90.7 3.9 %copy-start = (bf16[2048,768]{1,0:T(8,128)(2,1)S(1)}, bf16[2048,768]{1,0:T(8,128)(2,1)}, u32[]{:S(2)}) copy-start(bf16[2048,768]{1,0:T(8,128)(2,1)} %get-tuple-element.29) | copy-start | bytes 9437188
  94.7 1.8 %copy-start.1 = (f32[96,2304]{1,0:T(8,128)S(1)}, f32[96,2304]{1,0:T(8,128)}, u32[]{:S(2)}) copy-start(f32[96,2304]{1,0:T(8,128)} %get-tuple-element.30) | copy-start | bytes 2654212
  94.7 2.7 %copy-start.2 = (f32[96,768]{1,0:T(8,128)S(1)}, f32[96,768]{1,0:T(8,128)}, u32[]{:S(2)}) copy-start(f32[96,768]{1,0:T(8,128)} %get-tuple-element.31) | copy-start | bytes 884740
where the time goes:
time: 98.4 us; the launch traced here: 98.1 us
  Pallas kernels  84.8 us (86%)
  local copies, waits for them, and re-layouts  12.6 us (13%)
    pallas_call x1, Pallas kernels, block_step(): pl.pallas_call(kernel, out_shape=(jax.ShapeDtypeStruct((ROWS, WIDTH), BF1...  84.8 us
    unnamed x10, local copies, waits for them, and re-layouts  7.32 us
    slice x2, local copies, waits for them, and re-layouts, local_step(): return (out, gtok, gwqkv, gwout, gb[0], gb[1], dtemp[:, 0])  2.75 us

commit v1 on v0

v1 whole, which is shorter than its diff:
```python
import jax
import jax.numpy as jnp
from jax import lax
from jax.experimental import pallas as pl
from jax.experimental.pallas import tpu as pltpu
from jax.sharding import PartitionSpec as P

F32 = jnp.float32
BF16 = jnp.bfloat16
MESH = pl.DeviceIdType.MESH

ROWS = 2048
WIDTH = 768
HEADS = 16
HD = 48
GW = 384
GH = 8
BLK = 512
NBLK = ROWS // BLK
LNR = 32
PAIR = 192
TOT = 2304
MSG = (208, 192, 400)
MSG0 = (0, 208, 400)
SHARD = 96
CHUNKS = 8


def dot(a, b, ca, cb):
    return lax.dot_general(a, b, (((ca,), (cb,)), ((), ())), preferred_element_type=F32)


def kernel(temp_ref, gain_ref, bias_ref, x_hbm, dy_hbm, wqkv_hbm, wout_hbm,
           x_v, do_v, gwq_out, gwo_out, gb_out, dtemp_out,
           dy_v, u_v, ut_v, qkv_v, ot_v, w_v, wo_v,
           gm_v, sq_v, a_v, bd_v, dsq_v, row_v, pay_v, ar1, ar2, ar3, sum_v,
           gw_v, r1, r2, r3, du_v, gb_v, gbs_v, gbr_v,
           in_sem, w_sem,
           ar_send, ar_recv, s1_send, s1_recv, s2_send, s2_recv, s3_send, s3_recv, gb_send, gb_recv):
    dp = lax.axis_index('dp')
    me = lax.axis_index('sp')
    core = me % 2
    cx = (me // 2) % 2
    cy = me // 4
    partner = me + 1 - 2 * core
    xn = me + 2 - 4 * cx
    yn = me + 4 - 8 * cy
    first = xn + core * (yn - xn)
    second = yn + core * (xn - yn)
    ca = cx + core * (cy - cx)
    cb = cy + core * (cx - cy)

    def chip(a, b):
        return a * (1 + core) + b * (2 - core)

    def dev(i):
        return (dp, i)

    def remote(src, dst, ss, rs, to):
        return pltpu.make_async_remote_copy(src_ref=src, dst_ref=dst, send_sem=ss, recv_sem=rs,
                                            device_id=dev(to), device_id_type=MESH)

    barrier = pltpu.get_barrier_semaphore()
    for peer in (partner, xn, yn):
        pl.semaphore_signal(barrier, inc=1, device_id=dev(peer), device_id_type=MESH)

    def w_copy(g, p):
        return pltpu.make_async_copy(wqkv_hbm.at[:, pl.ds(p * WIDTH + g * GW, GW)],
                                     w_v.at[:, pl.ds((3 * g + p) * GW, GW)], w_sem.at[3 * g + p])

    wo_copy = pltpu.make_async_copy(wout_hbm, wo_v, w_sem.at[6])

    def x_copy(b):
        rows = pl.ds(b * BLK, BLK)
        return pltpu.make_async_copy(x_hbm.at[rows], x_v.at[rows], in_sem.at[0, b])

    def dy_copy(b):
        rows = pl.ds(b * BLK, BLK)
        return pltpu.make_async_copy(dy_hbm.at[rows], dy_v.at[rows], in_sem.at[1, b])

    x_copy(0).start()
    w_copy(0, 0).start()
    w_copy(0, 1).start()
    for b in range(1, NBLK):
        x_copy(b).start()
    w_copy(0, 2).start()
    wo_copy.start()
    for b in range(NBLK):
        dy_copy(b).start()
    for p in range(3):
        w_copy(1, p).start()

    gain = gain_ref[...].reshape(1, WIDTH)
    bias = bias_ref[...].reshape(1, WIDTH)

    def loop(f):
        def body(b, carry):
            f(b)
            return carry
        lax.fori_loop(0, NBLK, body, 0)

    def block(b):
        return pl.ds(pl.multiple_of(b * BLK, BLK), BLK)

    def normed_rows(r0):
        xf = x_v[pl.ds(r0, LNR), :].astype(F32)
        c = xf - jnp.mean(xf, axis=-1, keepdims=True)
        rstd = lax.rsqrt(jnp.mean(c * c, axis=-1, keepdims=True) + 1e-6)
        return c * rstd, rstd

    def norm_block(b):
        for i in range(BLK // LNR):
            r0 = b * BLK + i * LNR
            xhat, _ = normed_rows(r0)
            u_v[r0:r0 + LNR, :] = (xhat * gain + bias).astype(BF16)

    def sumsq(v):
        vf = v.astype(F32)
        return jnp.sum((vf * vf).reshape(BLK // 8, 8, GW), axis=0)

    def project(g, lo, hi, rows):
        res = dot(u_v[rows, :], w_v[:, (3 * g + lo) * GW:(3 * g + hi) * GW], 1, 0).astype(BF16)
        qkv_v[rows, (3 * g + lo) * GW:(3 * g + hi) * GW] = res
        if lo == 0:
            sq_v[g, 0] += sumsq(res[:, :GW])
            sq_v[g, 1] += sumsq(res[:, GW:2 * GW])

    def values_and_do(b):
        rows = block(b)
        project(0, 2, 3, rows)
        do_v[rows, :] = dot(dy_v[rows, :], wo_v[...], 1, 1).astype(BF16)
        ut_v[:, rows] = u_v[rows, :].T

    def pack(res, base):
        gm_v[...] = res
        lane = lax.broadcasted_iota(jnp.int32, (HD, 128), 1)

        def piece(h, to):
            lo = HD * h // 128 * 128
            hi = min(lo + 256, GW)
            v = gm_v[HD * h:HD * (h + 1), lo:hi]
            s = (to - (HD * h - lo)) % (hi - lo)
            if s:
                v = pltpu.roll(v, s, 1)
            return v[:, :128]
        for p in range(GH // 2):
            a = piece(2 * p, 0)
            d = piece(2 * p + 1, 64)
            both = jnp.where(lane < HD, a, jnp.where((lane >= 64) & (lane < 64 + HD), d, 0.0))
            pay_v[base + HD * p:base + HD * (p + 1), :] = both

    def gram(g, base):
        pack(dot(qkv_v[:, 3 * g * GW:(3 * g + 1) * GW], qkv_v[:, (3 * g + 1) * GW:(3 * g + 2) * GW], 0, 0), base)
        r0 = base + PAIR
        pay_v[r0:r0 + 16, :] = jnp.zeros((16, 128), F32)
        for p in range(2):
            row = jnp.sum(sq_v[g, p], axis=0, keepdims=True)
            for c in range(3):
                pay_v[r0 + 3 * p + c:r0 + 3 * p + c + 1, :] = row[:, 128 * c:128 * (c + 1)]

    def dgram(g, base):
        pack(dot(do_v[:, g * GW:(g + 1) * GW], qkv_v[:, (3 * g + 2) * GW:(3 * g + 3) * GW], 0, 0), base)

    held = {}

    def ar(m, k):
        half = MSG[m] // 2
        mine = pl.ds(pl.multiple_of(MSG0[m] + core * half, 8), half)
        theirs = pl.ds(pl.multiple_of(MSG0[m] + (1 - core) * half, 8), half)
        slot = pl.ds(MSG0[m] // 2, half)
        if k:
            held[m, k - 1].wait()
        if k == 1:
            pay_v[mine, :] = ar1[slot, :] + pay_v[mine, :]
        elif k == 2:
            pay_v[mine, :] = ar2[slot, :] + pay_v[mine, :]
        elif k == 3:
            sum_v[mine, :] = ar3[slot, :] + pay_v[mine, :]
        elif k == 4:
            return
        if k == 0:
            src, dst, to = pay_v.at[theirs], ar1.at[slot], partner
        elif k == 1:
            src, dst, to = pay_v.at[mine], ar2.at[slot], first
        elif k == 2:
            src, dst, to = pay_v.at[mine], ar3.at[slot], second
        else:
            src, dst, to = sum_v.at[mine], sum_v.at[mine], partner
        held[m, k] = remote(src, dst, ar_send.at[m, k], ar_recv.at[m, k], to)
        held[m, k].start()

    lane48 = lax.broadcasted_iota(jnp.int32, (HD, 128), 1)
    ok = lane48 < HD

    def place(v, h):
        wide = jnp.concatenate([v, jnp.zeros((v.shape[0], GW - 128), v.dtype)], axis=1)
        return pltpu.roll(wide, HD * h, 1) if h else wide

    def head_block(base, h):
        both = sum_v[base + HD * (h // 2):base + HD * (h // 2 + 1), :]
        if h % 2:
            both = pltpu.roll(both, 64, 1)
        return jnp.where(ok, both, 0.0)

    def attn(g, base):
        r0 = base + PAIR
        sqrow = jnp.concatenate([sum_v[r0 + c:r0 + c + 1, :] for c in range(3)], axis=1)
        skrow = jnp.concatenate([sum_v[r0 + 3 + c:r0 + 4 + c, :] for c in range(3)], axis=1)
        skwide = jnp.broadcast_to(skrow, (8, GW))
        for c in range(3):
            row_v[128 * c:128 * (c + 1), :] = jnp.broadcast_to(sqrow[:, 128 * c:128 * (c + 1)], (128, 128)).T
        for h in range(GH):
            hr = slice(HD * h, HD * (h + 1))
            skh = pltpu.roll(skwide, GW - HD * h, 1) if h else skwide
            skh = jnp.where(ok, jnp.broadcast_to(skh[:1, :128], (HD, 128)), 1.0)
            den = jnp.sqrt(row_v[hr, :]) * jnp.sqrt(skh)
            cosine = head_block(base, h) / den
            logit = jnp.where(ok, temp_ref[g * GH + h] * cosine, -jnp.inf)
            e = jnp.where(ok, jnp.exp(logit - jnp.max(logit, axis=1, keepdims=True)), 0.0)
            a = e / jnp.sum(e, axis=1, keepdims=True)
            a_v[0, hr, :] = a
            a_v[1, hr, :] = cosine
            a_v[2, hr, :] = den
            bd_v[0, hr, :] = place(a, h).astype(BF16)

    def attn_vjp(g, gbase, dbase):
        r0 = gbase + PAIR
        skrow = jnp.concatenate([sum_v[r0 + 3 + c:r0 + 4 + c, :] for c in range(3)], axis=1)
        dsk = jnp.zeros((8, GW), F32)
        dtemp = jnp.zeros((1, 128), F32)
        for h in range(GH):
            hr = slice(HD * h, HD * (h + 1))
            a, cosine, den = a_v[0, hr, :], a_v[1, hr, :], a_v[2, hr, :]
            da = head_block(dbase, h)
            ds = a * (da - jnp.sum(a * da, axis=1, keepdims=True))
            dt = jnp.sum(jnp.sum(ds * cosine, axis=1, keepdims=True), axis=0, keepdims=True)
            dtemp = jnp.where(lane48[:1] == g * GH + h, dt, dtemp)
            dcos = temp_ref[g * GH + h] * ds
            w = dcos * cosine
            row_v[hr, :] = -jnp.sum(w, axis=1, keepdims=True) / row_v[hr, :]
            dsk = dsk - place(jnp.broadcast_to(jnp.sum(w, axis=0, keepdims=True), (8, 128)), h)
            bd_v[1, hr, :] = place(dcos / den, h).astype(BF16)
        dsq_v[8:16, :] = dsk / skrow
        dsq_v[0:8, :] = jnp.concatenate(
            [row_v[128 * c:128 * (c + 1), :].T[:8] for c in range(3)], axis=1)
        if g == 0:
            dtemp_out[0:1, :] = dtemp
        else:
            dtemp_out[0:1, :] += dtemp

    def heads_v(g):
        def body(b):
            rows = block(b)
            cols = slice(g * GW, (g + 1) * GW)
            vc = slice((3 * g + 2) * GW, (3 * g + 3) * GW)
            a = bd_v[0]
            o = dot(qkv_v[rows, vc], a, 1, 1).astype(BF16)
            qkv_v[rows, vc] = dot(do_v[rows, cols], a, 1, 0).astype(BF16)
            do_v[rows, cols] = o
            ot_v[cols, rows] = o.T
        loop(body)

    def heads_qk(g):
        def body(b):
            rows = block(b)
            qc = slice(3 * g * GW, (3 * g + 1) * GW)
            kc = slice((3 * g + 1) * GW, (3 * g + 2) * GW)
            d = bd_v[1]
            q = qkv_v[rows, qc]
            k = qkv_v[rows, kc]
            dq = (dot(k, d, 1, 1) + q.astype(F32) * dsq_v[0:1, :]).astype(BF16)
            dk = (dot(q, d, 1, 0) + k.astype(F32) * dsq_v[8:9, :]).astype(BF16)
            qkv_v[rows, qc] = dq
            qkv_v[rows, kc] = dk
        loop(body)

    PART = {0: 2, 1: 0, 2: 1, 3: 5, 6: 3, 7: 4}

    def gw_chunks(ch, n):
        def half(m, carry):
            mr = pl.ds(pl.multiple_of(m * GW, GW), GW)
            if ch in PART:
                c0 = PART[ch] * GW
                res = dot(ut_v[mr, :], qkv_v[:, c0:c0 + n * GW], 1, 0)
            else:
                res = dot(ot_v[mr, :], dy_v[...], 1, 0)
            for i in range(n):
                gw_v[ch + i, pl.ds(2 * m, 2)] = res[:, i * GW:(i + 1) * GW].reshape(2, 2, SHARD, GW)
            return carry
        lax.fori_loop(0, 2, half, 0)

    def s1(ch):
        c = remote(gw_v.at[ch, :, 1 - core], r1.at[ch], s1_send.at[ch], s1_recv.at[ch], partner)
        c.start()
        held['s1', ch] = c

    def s2(ch):
        held['s1', ch].wait()
        for n, b in ((0, 1 - cb), (1, cb)):
            i = chip(1 - ca, b)
            r1[ch, i] += gw_v[ch, i, core]
            c = remote(r1.at[ch, i], r2.at[ch, b], s2_send.at[ch, b], s2_recv.at[ch, b], first)
            c.start()
            held['s2', ch, n] = c
        for b in (1 - cb, cb):
            i = chip(ca, b)
            r1[ch, i] += gw_v[ch, i, core]

    def s3(ch):
        held['s2', ch, 0].wait()
        r2[ch, 1 - cb] += r1[ch, chip(ca, 1 - cb)]
        c = remote(r2.at[ch, 1 - cb], r3.at[ch], s3_send.at[ch], s3_recv.at[ch], second)
        c.start()
        held['s3', ch] = c

    def s4(ch):
        held['s2', ch, 1].wait()
        held['s3', ch].wait()
        total = r3[ch] + (r2[ch, cb] + r1[ch, chip(ca, cb)])
        if ch in PART:
            g, p = divmod(PART[ch], 3)
            c0 = p * WIDTH + g * GW
            gwq_out[:, c0:c0 + GW] = total
        else:
            gwo_out[:, (ch - 4) * GW:(ch - 3) * GW] = total

    def final_dots(b):
        rows = slice(b * BLK, (b + 1) * BLK)
        du_v[b % 2] = dot(qkv_v[rows, :], w_v[...], 1, 1)
        do_v[rows, :] = (x_v[rows, :].astype(F32) + dot(do_v[rows, :], wo_v[...], 1, 0)).astype(BF16)

    def final_norm(b):
        dgain = jnp.zeros((8, WIDTH), F32)
        dbias = jnp.zeros((8, WIDTH), F32)
        for i in range(BLK // LNR):
            r0 = b * BLK + i * LNR
            sub = slice(r0, r0 + LNR)
            xhat, rstd = normed_rows(r0)
            du = du_v[b % 2, i * LNR:(i + 1) * LNR, :]
            dgain = dgain + jnp.sum((du * xhat).reshape(LNR // 8, 8, WIDTH), axis=0)
            dbias = dbias + jnp.sum(du.reshape(LNR // 8, 8, WIDTH), axis=0)
            dxh = du * gain
            m1 = jnp.mean(dxh, axis=-1, keepdims=True)
            m2 = jnp.mean(dxh * xhat, axis=-1, keepdims=True)
            dx = rstd * (dxh - m1 - xhat * m2)
            x_v[sub, :] = (dy_v[sub, :].astype(F32) + dx).astype(BF16)
        gb_v[0] += dgain
        gb_v[1] += dbias

    def gb_start(k):
        to = (partner, first, second)[k]
        c = remote(gbs_v.at[k], gbr_v.at[k], gb_send.at[k], gb_recv.at[k], to)
        c.start()
        held['gb', k] = c

    def gb_next(k):
        held['gb', k].wait()
        total = gbs_v[k] + gbr_v[k]
        if k < 2:
            gbs_v[k + 1] = total
            gb_start(k + 1)
        else:
            gb_out[...] = total

    sq_v[...] = jnp.zeros_like(sq_v)
    gb_v[...] = jnp.zeros_like(gb_v)
    dtemp_out[...] = jnp.zeros_like(dtemp_out)
    x_copy(0).wait()
    norm_block(0)
    w_copy(0, 0).wait()
    w_copy(0, 1).wait()
    for b in range(NBLK):
        if b + 1 < NBLK:
            x_copy(b + 1).wait()
            norm_block(b + 1)
        project(0, 0, 2, slice(b * BLK, (b + 1) * BLK))
    gram(0, MSG0[0])
    pl.semaphore_wait(barrier, 3)
    ar(0, 0)
    w_copy(0, 2).wait()
    wo_copy.wait()
    for b in range(NBLK):
        dy_copy(b).wait()
    loop(values_and_do)
    ar(0, 1)
    dgram(0, MSG0[1])
    ar(1, 0)
    for p in range(3):
        w_copy(1, p).wait()

    def project_1(b):
        project(1, 0, 3, block(b))
    lax.fori_loop(0, 2, lambda b, c: (project_1(b), c)[1], 0)
    ar(0, 2)
    ar(1, 1)
    lax.fori_loop(2, 4, lambda b, c: (project_1(b), c)[1], 0)
    gram(1, MSG0[2])
    ar(0, 3)
    ar(1, 2)
    dgram(1, MSG0[2] + PAIR + 16)
    ar(2, 0)
    ar(0, 4)
    attn(0, MSG0[0])
    ar(1, 3)
    ar(2, 1)
    heads_v(0)
    gw_chunks(0, 1)
    s1(0)
    ar(2, 2)
    ar(1, 4)
    attn_vjp(0, MSG0[0], MSG0[1])
    s2(0)
    heads_qk(0)
    ar(2, 3)
    gw_chunks(1, 2)
    s1(1)
    s1(2)
    ar(2, 4)
    attn(1, MSG0[2])
    s2(1)
    s2(2)
    s3(0)
    heads_v(1)
    gw_chunks(3, 1)
    s1(3)
    attn_vjp(1, MSG0[2], MSG0[2] + PAIR + 16)
    s2(3)
    s3(1)
    gw_chunks(4, 2)
    s1(4)
    s1(5)
    heads_qk(1)
    s2(4)
    s2(5)
    s3(2)
    gw_chunks(6, 2)
    s1(6)
    s1(7)
    final_dots(0)
    s2(6)
    s2(7)
    s3(3)
    final_norm(0)
    final_dots(1)
    s3(4)
    final_norm(1)
    final_dots(2)
    s3(5)
    final_norm(2)
    final_dots(3)
    s3(6)
    final_norm(3)
    gbs_v[0] = jnp.concatenate([jnp.sum(gb_v[i], axis=0, keepdims=True) for i in range(2)]
                               + [jnp.zeros((6, WIDTH), F32)], axis=0)
    gb_start(0)
    for ch in range(0, 4):
        s4(ch)
    gb_next(0)
    for ch in range(4, 6):
        s4(ch)
    gb_next(1)
    s3(7)
    s4(6)
    gb_next(2)
    s4(7)


def writer(out_v, gtok_v, gwq_v, gwo_v, gb_v, dtemp_v,
           out_hbm, gtok_hbm, gwq_hbm, gwo_hbm, gain_hbm, bias_hbm, dtemp_out, sem):
    pairs = [(gtok_v, gtok_hbm), (out_v, out_hbm), (gwq_v, gwq_hbm), (gwo_v, gwo_hbm),
             (gb_v.at[0], gain_hbm), (gb_v.at[1], bias_hbm)]
    copies = [pltpu.make_async_copy(src, dst, sem.at[i]) for i, (src, dst) in enumerate(pairs)]
    for c in copies:
        c.start()
    dtemp_out[...] = dtemp_v[0, :HEADS]
    for c in copies:
        c.wait()


def block_step(x, dy, ln_gain, ln_bias, w_qkv, w_out, temperature):
    hbm = pl.BlockSpec(memory_space=pl.ANY)
    vmem = pl.BlockSpec(memory_space=pltpu.VMEM)
    smem = pl.BlockSpec(memory_space=pltpu.SMEM)
    dma = pltpu.SemaphoreType.DMA
    gtok, out, gwq, gwo, gb, dtemp = pl.pallas_call(
        kernel,
        out_shape=(
            pltpu.VMEM((ROWS, WIDTH), BF16),
            pltpu.VMEM((ROWS, WIDTH), BF16),
            pltpu.VMEM((SHARD, TOT), F32),
            pltpu.VMEM((SHARD, WIDTH), F32),
            pltpu.VMEM((8, WIDTH), F32),
            pltpu.VMEM((8, 128), F32),
        ),
        in_specs=[smem, vmem, vmem, hbm, hbm, hbm, hbm],
        out_specs=(vmem,) * 6,
        scratch_shapes=[
            pltpu.VMEM((ROWS, WIDTH), BF16),
            pltpu.VMEM((ROWS, WIDTH), BF16),
            pltpu.VMEM((WIDTH, ROWS), BF16),
            pltpu.VMEM((ROWS, TOT), BF16),
            pltpu.VMEM((WIDTH, ROWS), BF16),
            pltpu.VMEM((WIDTH, TOT), BF16),
            pltpu.VMEM((WIDTH, WIDTH), BF16),
            pltpu.VMEM((GW, GW), F32),
            pltpu.VMEM((2, 2, 8, GW), F32),
            pltpu.VMEM((3, GW, 128), F32),
            pltpu.VMEM((2, GW, GW), BF16),
            pltpu.VMEM((16, GW), F32),
            pltpu.VMEM((GW, 128), F32),
            pltpu.VMEM((800, 128), F32),
            pltpu.VMEM((400, 128), F32),
            pltpu.VMEM((400, 128), F32),
            pltpu.VMEM((400, 128), F32),
            pltpu.VMEM((800, 128), F32),
            pltpu.VMEM((CHUNKS, 4, 2, SHARD, GW), F32),
            pltpu.VMEM((CHUNKS, 4, SHARD, GW), F32),
            pltpu.VMEM((CHUNKS, 2, SHARD, GW), F32),
            pltpu.VMEM((CHUNKS, SHARD, GW), F32),
            pltpu.VMEM((2, BLK, WIDTH), F32),
            pltpu.VMEM((2, 8, WIDTH), F32),
            pltpu.VMEM((3, 8, WIDTH), F32),
            pltpu.VMEM((3, 8, WIDTH), F32),
            dma((2, NBLK)), dma((7,)),
            dma((3, 4)), dma((3, 4)),
            dma((CHUNKS,)), dma((CHUNKS,)),
            dma((CHUNKS, 2)), dma((CHUNKS, 2)),
            dma((CHUNKS,)), dma((CHUNKS,)),
            dma((3,)), dma((3,)),
        ],
        compiler_params=pltpu.CompilerParams(
            collective_id=0, has_side_effects=True, vmem_limit_bytes=58000000),
    )(temperature, ln_gain, ln_bias, x, dy, w_qkv, w_out)
    return pl.pallas_call(
        writer,
        out_shape=(
            jax.ShapeDtypeStruct((ROWS, WIDTH), BF16),
            jax.ShapeDtypeStruct((ROWS, WIDTH), BF16),
            jax.ShapeDtypeStruct((SHARD, TOT), F32),
            jax.ShapeDtypeStruct((SHARD, WIDTH), F32),
            jax.ShapeDtypeStruct((WIDTH,), F32),
            jax.ShapeDtypeStruct((WIDTH,), F32),
            jax.ShapeDtypeStruct((HEADS,), F32),
        ),
        in_specs=[vmem] * 6,
        out_specs=(hbm,) * 6 + (vmem,),
        scratch_shapes=[dma((6,))],
        compiler_params=pltpu.CompilerParams(vmem_limit_bytes=1000000),
    )(out, gtok, gwq, gwo, gb, dtemp)


def solution(mesh):
    row_spec = P(('dp', 'sp'), None)
    part_spec = P('dp')
    full_spec = P()

    return jax.shard_map(block_step, mesh=mesh,
                         in_specs=(row_spec, row_spec, full_spec, full_spec, full_spec, full_spec, full_spec),
                         out_specs=(row_spec, row_spec, row_spec, row_spec, part_spec, part_spec, part_spec),
                         check_vma=False)
```

time: 98.4 us -> 84.5 us (0.86)
  local copies, waits for them, and re-layouts: 12.6 us -> 0 us
  Pallas kernels: 84.8 us -> 83.5 us
    unnamed x10 -> x0, local copies, waits for them, and re-layouts: 7.32 us -> none
    slice x2 -> x0, local copies, waits for them, and re-layouts: 2.75 us -> none  [local_step(): return (out, gtok, gwqkv, gwout, gb[0], gb[1], dtemp[:, 0])]
    reshape x2 -> x0, local copies, waits for them, and re-layouts: 2.53 us -> none  [the longest x1 1.27 us: block_step(): ln_gain.reshape(1, WIDTH)]
    pallas_call x1 -> x2, Pallas kernels: 84.8 us -> 83.5 us  [the longest x1 79.9 us: block_step(): pl.pallas_call(kernel, out_shape=(pltpu.VMEM((ROWS, WIDTH), BF16), pltpu....]
where the time goes in v1:
time: 84.5 us; the launch traced here: 84.3 us
  Pallas kernels  83.5 us (99%)
    pallas_call x1, Pallas kernels, block_step(): pl.pallas_call(kernel, out_shape=(pltpu.VMEM((ROWS, WIDTH), BF16), pltpu....  79.9 us
    pallas_call x1, Pallas kernels, block_step(): pl.pallas_call(writer, out_shape=(jax.ShapeDtypeStruct((ROWS, WIDTH), BF1...  3.62 us

profile of v1, /device:TPU:0, one launch (start us, length us, event | category | flops | bytes accessed | tf_op | source)
XLA Modules:
  0.0 84.3 jit_solution(15047288588639330313)
XLA Ops:
  0.6 79.9 %shard_map.126 = (bf16[2048,768]{1,0:T(8,128)(2,1)S(1)}, bf16[2048,768]{1,0:T(8,128)(2,1)S(1)}, f32[96,2304]{1,0:T(8,128)S(1)}, f32[96,768]{1,0:T(8,128)S(1)}, f...) custom-call(f32[16]{0:T(128)} %temp_ref.1, f32[768]{0:T(1024)} %gain_ref.1, f32[768]{0:T(1024)} %bias_ref.1, ...), custom_call_target="tpu_custom_call" | custom-call | tf_op jit(solution)/shard_map/pallas_call | solution.py:485
  80.5 3.6 %shard_map.127 = (bf16[2048,768]{1,0:T(8,128)(2,1)}, bf16[2048,768]{1,0:T(8,128)(2,1)}, f32[96,2304]{1,0:T(8,128)}, f32[96,768]{1,0:T(8,128)}, f32[768]{0:T(1024)}, /*index=5*/f32[768]{0:T(1024)}, f32[16]{0:T(128)}) custom-call(bf16[2048,768]{1,0:T(8,128)(2,1)S(1)} %get-tuple-element.13.out_v, bf16[2048,768]{1,0:T(8,128)(2,1)S(1)} %get-tuple-element.14.gtok_v, ...), custom_call_target="tpu_custom_call" | custom-call | tf_op jit(solution)/shard_map/pallas_call | solution.py:534

commit v2 on v1

v2 whole, which is shorter than its diff:
```python
import jax
import jax.numpy as jnp
from jax import lax
from jax.experimental import pallas as pl
from jax.experimental.pallas import tpu as pltpu
from jax.sharding import PartitionSpec as P

F32 = jnp.float32
BF16 = jnp.bfloat16
MESH = pl.DeviceIdType.MESH

ROWS = 2048
WIDTH = 768
HEADS = 16
HD = 48
GW = 384
GH = 8
BLK = 512
NBLK = ROWS // BLK
BIG = 1024
FINE = 256
NFINE = ROWS // FINE
LNR = 32
PAIR = 192
TOT = 2304
LANES = 128
TILE = 256
SPLIT = 5
MSG = (208, 208, 192, 192)
MSG0 = (0, 208, 416, 608)
PAY = 800
SLOTS = 4
ORDER = ((0, 1, 2), (4, 5, 3))
SHARD = 96
CHUNKS = 8


def dot(a, b, ca, cb):
    return lax.dot_general(a, b, (((ca,), (cb,)), ((), ())), preferred_element_type=F32)


def kernel(temp_ref, gain_ref, bias_ref, x_hbm, dy_hbm, wqkv_hbm, wout_hbm,
           x_v, do_v, gwq_out, gwo_out, gb_out, dtemp_out,
           dy_v, u_v, ut_v, qkv_v, v_v, ot_v, w_v, wo_v,
           gm_v, sq_v, a_v, bd_v, dsq_v, row_v, pay_v, ar1, ar2, ar3, sum_v,
           gw_v, r1, r2, r3, du0, du1, gb_v, gbs_v, gbr_v,
           in_sem, w_sem, x_sem,
           ar_send, ar_recv, s1_send, s1_recv, s2_send, s2_recv, s3_send, s3_recv, gb_send, gb_recv):
    dp = lax.axis_index('dp')
    me = lax.axis_index('sp')
    core = me % 2
    cx = (me // 2) % 2
    cy = me // 4
    partner = me + 1 - 2 * core
    xn = me + 2 - 4 * cx
    yn = me + 4 - 8 * cy
    first = xn + core * (yn - xn)
    second = yn + core * (xn - yn)
    diagonal = xn + 4 - 8 * cy
    ca = cx + core * (cy - cx)
    cb = cy + core * (cx - cy)

    def chip(a, b):
        return a * (1 + core) + b * (2 - core)

    def dev(i):
        return (dp, i)

    def remote(src, dst, ss, rs, to):
        return pltpu.make_async_remote_copy(src_ref=src, dst_ref=dst, send_sem=ss, recv_sem=rs,
                                            device_id=dev(to), device_id_type=MESH)

    barrier = pltpu.get_barrier_semaphore()
    for peer in (partner, xn, yn, diagonal):
        pl.semaphore_signal(barrier, inc=1, device_id=dev(peer), device_id_type=MESH)

    def cols(g, p):
        return slice(ORDER[g][p] * GW, (ORDER[g][p] + 1) * GW)

    def w_copy(g, p):
        return pltpu.make_async_copy(wqkv_hbm.at[:, pl.ds(p * WIDTH + g * GW, GW)],
                                     w_v.at[:, pl.ds(ORDER[g][p] * GW, GW)], w_sem.at[ORDER[g][p]])

    wo_copy = pltpu.make_async_copy(wout_hbm, wo_v, w_sem.at[6])

    def x_copy(b):
        rows = pl.ds(b * FINE, FINE)
        return pltpu.make_async_copy(x_hbm.at[rows], x_v.at[rows], x_sem.at[b])

    def dy_copy(b):
        rows = pl.ds(b * BLK, BLK)
        return pltpu.make_async_copy(dy_hbm.at[rows], dy_v.at[rows], in_sem.at[b])

    for b in range(2):
        x_copy(b).start()
    for p in range(2):
        w_copy(0, p).start()
    for b in range(2, NFINE):
        x_copy(b).start()
    for p in range(2):
        w_copy(1, p).start()
    for g in range(2):
        w_copy(g, 2).start()
    wo_copy.start()
    for b in range(NBLK):
        dy_copy(b).start()

    gain = gain_ref[...].reshape(1, WIDTH)
    bias = bias_ref[...].reshape(1, WIDTH)

    def loop(f, hooks=(), lo=0, hi=NBLK):
        def body(b, carry):
            f(b)
            for at, hook in hooks:
                pl.when(b == at)(hook)
            return carry
        lax.fori_loop(lo, hi, body, 0)

    def block(b, n=BLK):
        return pl.ds(pl.multiple_of(b * n, n), n)

    def normed_rows(r0):
        xf = x_v[pl.ds(r0, LNR), :].astype(F32)
        c = xf - jnp.mean(xf, axis=-1, keepdims=True)
        rstd = lax.rsqrt(jnp.mean(c * c, axis=-1, keepdims=True) + 1e-6)
        return c * rstd, rstd

    def norm_block(b):
        for r0 in range(b * BLK, (b + 1) * BLK, LNR):
            if b == 0 and r0 % FINE == 0:
                x_copy(r0 // FINE).wait()
            xhat, _ = normed_rows(r0)
            u_v[r0:r0 + LNR, :] = (xhat * gain + bias).astype(BF16)

    def sumsq(v):
        vf = v.astype(F32)
        return jnp.sum((vf * vf).reshape(-1, 8, GW), axis=0)

    def project(n, rows):
        c = slice(n * WIDTH, (n + 1) * WIDTH)
        res = dot(u_v[rows, :], w_v[:, c], 1, 0).astype(BF16)
        if n == 1:
            v_v[rows, :] = res
        else:
            qkv_v[rows, c] = res
            sq_v[n // 2, 0] += sumsq(res[:, :GW])
            sq_v[n // 2, 1] += sumsq(res[:, GW:])

    def values_and_do(b):
        rows = block(b)
        project(1, rows)
        do_v[rows, :] = dot(dy_v[rows, :], wo_v[...], 1, 1).astype(BF16)
        ut_v[:, rows] = u_v[rows, :].T

    lane48 = lax.broadcasted_iota(jnp.int32, (HD, LANES), 1)
    ok = lane48 < HD

    def local(h):
        t = int(h >= SPLIT)
        return t, HD * h - LANES * t

    def pack(left, lc, right, rc, base):
        for t in range(2):
            off = LANES * t
            gm_v[t] = dot(left[:, lc + off:lc + off + TILE], right[:, rc + off:rc + off + TILE], 0, 0)

        def piece(h, to):
            t, r = local(h)
            lo = r // LANES * LANES
            n = LANES if r + HD <= lo + LANES else TILE
            v = gm_v[t, r:r + HD, lo:lo + n]
            move = (to - (r - lo)) % n
            if move:
                v = pltpu.roll(v, move, 1)
            return v[:, :LANES]
        for p in range(GH // 2):
            a = piece(2 * p, 0)
            d = piece(2 * p + 1, LANES // 2)
            side = lane48 - LANES // 2
            both = jnp.where(ok, a, jnp.where((side >= 0) & (side < HD), d, 0.0))
            pay_v[base + HD * p:base + HD * (p + 1), :] = both

    def gram(g):
        pack(qkv_v, cols(g, 0).start, qkv_v, cols(g, 1).start, MSG0[g])
        r0 = MSG0[g] + PAIR
        pay_v[r0:r0 + 16, :] = jnp.zeros((16, LANES), F32)
        for p in range(2):
            row = jnp.sum(sq_v[g, p], axis=0, keepdims=True)
            for c in range(3):
                pay_v[r0 + 3 * p + c:r0 + 3 * p + c + 1, :] = row[:, LANES * c:LANES * (c + 1)]

    def dgram(g):
        pack(do_v, g * GW, v_v, g * GW, MSG0[2 + g])

    held = {}

    def ar(m, k):
        half = MSG[m] // 2
        mine = pl.ds(pl.multiple_of(MSG0[m] + core * half, 8), half)
        theirs = pl.ds(pl.multiple_of(MSG0[m] + (1 - core) * half, 8), half)
        slot = pl.ds(MSG0[m] // 2, half)
        steps = ((pay_v.at[theirs], ar1.at[slot], partner), (pay_v.at[mine], ar2.at[slot], first),
                 (pay_v.at[mine], ar3.at[slot], second), (sum_v.at[mine], sum_v.at[mine], partner))

        def copy(n):
            src, dst, to = steps[n]
            return remote(src, dst, ar_send.at[m, n], ar_recv.at[m, n], to)
        if k:
            copy(k - 1).wait()
        if k == 1:
            pay_v[mine, :] = ar1[slot, :] + pay_v[mine, :]
        elif k == 2:
            pay_v[mine, :] = ar2[slot, :] + pay_v[mine, :]
        elif k == 3:
            sum_v[mine, :] = ar3[slot, :] + pay_v[mine, :]
        if k < 4:
            copy(k).start()

    def hook(*steps):
        def run():
            for m, k in steps:
                ar(m, k)
        return run

    def place(v, at, n):
        wide = jnp.concatenate([v, jnp.zeros((v.shape[0], n - LANES), v.dtype)], axis=1)
        return pltpu.roll(wide, at, 1) if at else wide

    def put(g, k, h, v):
        t, r = local(h)
        bd_v[g, k, t, r:r + HD, :] = place(v, r, TILE).astype(BF16)

    def head_block(base, h):
        r0 = base + HD * (h // 2)
        both = sum_v[r0:r0 + HD, :]
        if h % 2:
            both = pltpu.roll(both, LANES // 2, 1)
        return jnp.where(ok, both, 0.0)

    def sums(g, p):
        r0 = MSG0[g] + PAIR + 3 * p
        return jnp.concatenate([sum_v[r0 + c:r0 + c + 1, :] for c in range(3)], axis=1)

    def attn(g):
        sqrow = sums(g, 0)
        skwide = jnp.broadcast_to(sums(g, 1), (8, GW))
        for c in range(3):
            lanes = slice(LANES * c, LANES * (c + 1))
            row_v[g, lanes, :] = jnp.broadcast_to(sqrow[:, lanes], (LANES, LANES)).T
        for h in range(GH):
            hr = slice(HD * h, HD * (h + 1))
            skh = pltpu.roll(skwide, GW - HD * h, 1) if h else skwide
            skh = jnp.where(ok, jnp.broadcast_to(skh[:1, :LANES], (HD, LANES)), 1.0)
            den = jnp.sqrt(row_v[g, hr, :]) * jnp.sqrt(skh)
            cosine = head_block(MSG0[g], h) / den
            logit = jnp.where(ok, temp_ref[g * GH + h] * cosine, -jnp.inf)
            e = jnp.where(ok, jnp.exp(logit - jnp.max(logit, axis=1, keepdims=True)), 0.0)
            a = e / jnp.sum(e, axis=1, keepdims=True)
            for i, v in enumerate((a, cosine, den)):
                a_v[g, i, hr, :] = v
            put(g, 0, h, a)

    def attn_vjp(g):
        dsk = jnp.zeros((8, GW), F32)
        dtemp = jnp.zeros((1, LANES), F32)
        for h in range(GH):
            hr = slice(HD * h, HD * (h + 1))
            a, cosine, den = [a_v[g, i, hr, :] for i in range(3)]
            da = head_block(MSG0[2 + g], h)
            ds = a * (da - jnp.sum(a * da, axis=1, keepdims=True))
            dt = jnp.sum(jnp.sum(ds * cosine, axis=1, keepdims=True), axis=0, keepdims=True)
            dtemp = jnp.where(lane48[:1] == g * GH + h, dt, dtemp)
            dcos = temp_ref[g * GH + h] * ds
            w = dcos * cosine
            row_v[g, hr, :] = -jnp.sum(w, axis=1, keepdims=True) / row_v[g, hr, :]
            dsk = dsk - place(jnp.broadcast_to(jnp.sum(w, axis=0, keepdims=True), (8, LANES)), HD * h, GW)
            put(g, 1, h, dcos / den)
        dsq_v[g, 1] = dsk / sums(g, 1)
        dsq_v[g, 0] = jnp.concatenate([row_v[g, LANES * c:LANES * (c + 1), :].T[:8] for c in range(3)], axis=1)
        dtemp_out[:1, :] += dtemp

    def head_dot(g, x, k, c):
        lo = dot(x[:, :TILE], bd_v[g, k, 0], 1, c)
        hi = dot(x[:, LANES:], bd_v[g, k, 1], 1, c)
        return jnp.concatenate([lo[:, :LANES], lo[:, LANES:] + hi[:, :LANES], hi[:, LANES:]], axis=1)

    def heads_v(g):
        def body(b):
            rows = block(b, BIG)
            oc = slice(g * GW, (g + 1) * GW)
            qkv_v[rows, cols(g, 2)] = head_dot(g, do_v[rows, oc], 0, 0).astype(BF16)
            o = head_dot(g, v_v[rows, oc], 0, 1).astype(BF16)
            u_v[rows, oc] = o
            ot_v[oc, rows] = o.T
        loop(body, hi=ROWS // BIG)

    def heads_qk(g):
        def body(b):
            rows = block(b, BIG)
            q = qkv_v[rows, cols(g, 0)]
            k = qkv_v[rows, cols(g, 1)]
            dq = head_dot(g, k, 1, 1) + q.astype(F32) * dsq_v[g, 0, :1, :]
            dk = head_dot(g, q, 1, 0) + k.astype(F32) * dsq_v[g, 1, :1, :]
            qkv_v[rows, cols(g, 0)] = dq.astype(BF16)
            qkv_v[rows, cols(g, 1)] = dk.astype(BF16)
        loop(body, hi=ROWS // BIG)

    PART = ((0, 2), (1, 2), None, None, (0, 0), (0, 1), (1, 0), (1, 1))

    def s1(k, m):
        two = pl.ds(2 * m, 2)
        return remote(gw_v.at[k % SLOTS, two, 1 - core], r1.at[k, two], s1_send.at[k, m], s1_recv.at[k, m], partner)

    def gw_chunks(ch, n):
        def half(m, carry):
            mr = pl.ds(pl.multiple_of(m * GW, GW), GW)
            if PART[ch]:
                c0 = cols(*PART[ch]).start
                res = dot(ut_v[mr, :], qkv_v[:, c0:c0 + n * GW], 1, 0)
            else:
                res = dot(ot_v[mr, :], dy_v[...], 1, 0)
            for i in range(n):
                gw_v[(ch + i) % SLOTS, pl.ds(2 * m, 2)] = res[:, i * GW:(i + 1) * GW].reshape(2, 2, SHARD, GW)
            for i in range(n):
                s1(ch + i, m).start()
            return carry
        lax.fori_loop(0, 2, half, 0)

    def s2_copy(ch, b):
        return remote(r1.at[ch, chip(1 - ca, b)], r2.at[ch, b], s2_send.at[ch, b], s2_recv.at[ch, b], first)

    def s2_near(ch, b):
        i = chip(ca, b)
        r1[ch, i] += gw_v[ch % SLOTS, i, core]

    def s2_far(ch, b):
        i = chip(1 - ca, b)
        r1[ch, i] += gw_v[ch % SLOTS, i, core]
        s2_copy(ch, b).start()

    def s2(ch, last=False):
        for m in range(2):
            s1(ch, m).wait()
        s2_far(ch, 1 - cb)
        if not last:
            s2_far(ch, cb)
        s2_near(ch, 1 - cb)
        s2_near(ch, cb)

    def s3_copy(ch):
        return remote(r2.at[ch, 1 - cb], r3.at[ch], s3_send.at[ch], s3_recv.at[ch], second)

    def s3(ch):
        s2_copy(ch, 1 - cb).wait()
        r2[ch, 1 - cb] += r1[ch, chip(ca, 1 - cb)]
        s3_copy(ch).start()

    def s4(ch):
        s2_copy(ch, cb).wait()
        s3_copy(ch).wait()
        total = r3[ch] + (r2[ch, cb] + r1[ch, chip(ca, cb)])
        if PART[ch]:
            g, p = PART[ch]
            c0 = p * WIDTH + g * GW
            gwq_out[:, c0:c0 + GW] = total
        else:
            gwo_out[:, (ch - 2) * GW:(ch - 1) * GW] = total

    def out_tokens(b):
        rows = block(b)
        do_v[rows, :] = (x_v[rows, :].astype(F32) + dot(u_v[rows, :], wo_v[...], 1, 0)).astype(BF16)

    def final_dots(b):
        (du0, du1)[b % 2][...] = dot(qkv_v[b * BLK:(b + 1) * BLK, :], w_v[...], 1, 1)

    def final_norm(b):
        du_ref = (du0, du1)[b % 2]
        dgain = jnp.zeros((8, WIDTH), F32)
        dbias = jnp.zeros((8, WIDTH), F32)
        for i in range(0, BLK, LNR):
            sub = slice(b * BLK + i, b * BLK + i + LNR)
            xhat, rstd = normed_rows(b * BLK + i)
            du = du_ref[i:i + LNR, :]
            dgain = dgain + jnp.sum((du * xhat).reshape(-1, 8, WIDTH), axis=0)
            dbias = dbias + jnp.sum(du.reshape(-1, 8, WIDTH), axis=0)
            dxh = du * gain
            m1 = jnp.mean(dxh, axis=-1, keepdims=True)
            m2 = jnp.mean(dxh * xhat, axis=-1, keepdims=True)
            dx = rstd * (dxh - m1 - xhat * m2)
            x_v[sub, :] = (dy_v[sub, :].astype(F32) + dx).astype(BF16)
        gb_v[0] += dgain
        gb_v[1] += dbias

    def last_step(b):
        if b < NBLK:
            final_dots(b)
        if b:
            final_norm(b - 1)

    def gb_start():
        both = [jnp.sum(gb_v[i], axis=0, keepdims=True) for i in range(2)]
        gbs_v[0] = jnp.concatenate(both + [jnp.zeros((6, WIDTH), F32)], axis=0)
        c = remote(gbs_v.at[0], gbs_v.at[1], gb_send.at[3], gb_recv.at[3], partner)
        c.start()
        held['gb', 3] = c

    def gb_chips():
        held['gb', 3].wait()
        here = me // 2
        gbr_v[here] = gbs_v[0] + gbs_v[1]
        for k, to in enumerate((first, second, diagonal)):
            c = remote(gbr_v.at[here], gbr_v.at[here], gb_send.at[k], gb_recv.at[k], to)
            c.start()
            held['gb', k] = c

    def gb_end():
        for k in range(3):
            held['gb', k].wait()
        gb_out[...] = (gbr_v[0] + gbr_v[1]) + (gbr_v[2] + gbr_v[3])

    for ref in (sq_v, gb_v, dtemp_out, bd_v):
        ref[...] = jnp.zeros_like(ref)
    def first_step(b):
        if b + 1 < NBLK:
            for i in range(2):
                x_copy(2 * (b + 1) + i).wait()
            norm_block(b + 1)
        project(0, slice(b * BLK, (b + 1) * BLK))

    norm_block(0)
    for p in range(2):
        w_copy(0, p).wait()
    for b in range(NBLK):
        first_step(b)
    gram(0)
    pl.semaphore_wait(barrier, 4)
    ar(0, 0)
    for p in range(2):
        w_copy(1, p).wait()
    loop(lambda b: project(2, block(b)), ((1, hook((0, 1))),))
    gram(1)
    ar(1, 0)
    for g in range(2):
        w_copy(g, 2).wait()
    wo_copy.wait()
    for b in range(NBLK):
        dy_copy(b).wait()
    loop(values_and_do, ((0, hook((0, 2), (1, 1))), (2, hook((0, 3))), (3, hook((1, 2), (0, 4)))))
    attn(0)
    heads_v(0)
    ar(1, 3)
    gw_chunks(0, 1)
    dgram(0)
    ar(2, 0)
    ar(1, 4)
    attn(1)
    ar(2, 1)
    s2(0)
    heads_v(1)
    gw_chunks(1, 1)
    ar(2, 2)
    dgram(1)
    ar(3, 0)
    s2(1)
    ar(3, 1)
    s3(0)
    gw_chunks(2, 2)
    ar(2, 3)

    def mid():
        s2(2)
        s2(3)

    def late():
        ar(2, 4)
        s3(1)

    loop(out_tokens, ((0, mid), (1, late)), hi=NBLK - 1)
    attn_vjp(0)
    heads_qk(0)
    ar(3, 2)
    gw_chunks(4, 2)
    out_tokens(NBLK - 1)
    ar(3, 3)
    s2(4)
    s2(5)
    s3(2)
    ar(3, 4)
    attn_vjp(1)
    heads_qk(1)
    gw_chunks(6, 2)
    s3(3)
    last_step(0)
    s2(6)
    s2(7, True)
    s3(4)
    for b in range(1, NBLK + 1):
        last_step(b)
        if b in (2, 3):
            s3(3 + b)
    gb_start()
    for ch in range(4):
        s4(ch)
    gb_chips()
    s2_far(7, cb)
    s4(4)
    s3(7)
    s4(5)
    s4(6)
    gb_end()
    s4(7)


def writer(out_v, gtok_v, gwq_v, gwo_v, gb_v, dtemp_v,
           out_hbm, gtok_hbm, gwq_hbm, gwo_hbm, gain_hbm, bias_hbm, dtemp_out, sem):
    pairs = [(gtok_v, gtok_hbm), (out_v, out_hbm), (gwq_v, gwq_hbm), (gwo_v, gwo_hbm),
             (gb_v.at[0], gain_hbm), (gb_v.at[1], bias_hbm)]
    copies = [pltpu.make_async_copy(src, dst, sem.at[i]) for i, (src, dst) in enumerate(pairs)]
    for c in copies:
        c.start()
    dtemp_out[...] = dtemp_v[0, :HEADS]
    for c in copies:
        c.wait()


def block_step(x, dy, ln_gain, ln_bias, w_qkv, w_out, temperature):
    hbm = pl.BlockSpec(memory_space=pl.ANY)
    vmem = pl.BlockSpec(memory_space=pltpu.VMEM)
    smem = pl.BlockSpec(memory_space=pltpu.SMEM)
    dma = pltpu.SemaphoreType.DMA
    gtok, out, gwq, gwo, gb, dtemp = pl.pallas_call(
        kernel,
        out_shape=(
            pltpu.VMEM((ROWS, WIDTH), BF16),
            pltpu.VMEM((ROWS, WIDTH), BF16),
            pltpu.VMEM((SHARD, TOT), F32),
            pltpu.VMEM((SHARD, WIDTH), F32),
            pltpu.VMEM((8, WIDTH), F32),
            pltpu.VMEM((8, 128), F32),
        ),
        in_specs=[smem, vmem, vmem, hbm, hbm, hbm, hbm],
        out_specs=(vmem,) * 6,
        scratch_shapes=[
            pltpu.VMEM((ROWS, WIDTH), BF16),
            pltpu.VMEM((ROWS, WIDTH), BF16),
            pltpu.VMEM((WIDTH, ROWS), BF16),
            pltpu.VMEM((ROWS, TOT), BF16),
            pltpu.VMEM((ROWS, WIDTH), BF16),
            pltpu.VMEM((WIDTH, ROWS), BF16),
            pltpu.VMEM((WIDTH, TOT), BF16),
            pltpu.VMEM((WIDTH, WIDTH), BF16),
            pltpu.VMEM((2, TILE, TILE), F32),
            pltpu.VMEM((2, 2, 8, GW), F32),
            pltpu.VMEM((2, 3, GW, LANES), F32),
            pltpu.VMEM((2, 2, 2, TILE, TILE), BF16),
            pltpu.VMEM((2, 2, 8, GW), F32),
            pltpu.VMEM((2, GW, LANES), F32),
            pltpu.VMEM((PAY, LANES), F32),
            pltpu.VMEM((PAY // 2, LANES), F32),
            pltpu.VMEM((PAY // 2, LANES), F32),
            pltpu.VMEM((PAY // 2, LANES), F32),
            pltpu.VMEM((PAY, LANES), F32),
            pltpu.VMEM((SLOTS, 4, 2, SHARD, GW), F32),
            pltpu.VMEM((CHUNKS, 4, SHARD, GW), F32),
            pltpu.VMEM((CHUNKS, 2, SHARD, GW), F32),
            pltpu.VMEM((CHUNKS, SHARD, GW), F32),
            pltpu.VMEM((BLK, WIDTH), F32),
            pltpu.VMEM((BLK, WIDTH), F32),
            pltpu.VMEM((2, 8, WIDTH), F32),
            pltpu.VMEM((2, 8, WIDTH), F32),
            pltpu.VMEM((4, 8, WIDTH), F32),
            dma((NBLK,)), dma((7,)), dma((NFINE,)),
            dma((4, 4)), dma((4, 4)),
            dma((CHUNKS, 2)), dma((CHUNKS, 2)),
            dma((CHUNKS, 2)), dma((CHUNKS, 2)),
            dma((CHUNKS,)), dma((CHUNKS,)),
            dma((4,)), dma((4,)),
        ],
        compiler_params=pltpu.CompilerParams(
            collective_id=0, has_side_effects=True, vmem_limit_bytes=59400000),
    )(temperature, ln_gain, ln_bias, x, dy, w_qkv, w_out)
    return pl.pallas_call(
        writer,
        out_shape=(
            jax.ShapeDtypeStruct((ROWS, WIDTH), BF16),
            jax.ShapeDtypeStruct((ROWS, WIDTH), BF16),
            jax.ShapeDtypeStruct((SHARD, TOT), F32),
            jax.ShapeDtypeStruct((SHARD, WIDTH), F32),
            jax.ShapeDtypeStruct((WIDTH,), F32),
            jax.ShapeDtypeStruct((WIDTH,), F32),
            jax.ShapeDtypeStruct((HEADS,), F32),
        ),
        in_specs=[vmem] * 6,
        out_specs=(hbm,) * 6 + (vmem,),
        scratch_shapes=[dma((6,))],
        compiler_params=pltpu.CompilerParams(vmem_limit_bytes=1000000),
    )(out, gtok, gwq, gwo, gb, dtemp)


def solution(mesh):
    row_spec = P(('dp', 'sp'), None)
    part_spec = P('dp')
    full_spec = P()

    return jax.shard_map(block_step, mesh=mesh,
                         in_specs=(row_spec, row_spec, full_spec, full_spec, full_spec, full_spec, full_spec),
                         out_specs=(row_spec, row_spec, row_spec, row_spec, part_spec, part_spec, part_spec),
                         check_vma=False)
```

time: 84.5 us -> 77.1 us (0.912)
  Pallas kernels: 83.5 us -> 76.1 us
    pallas_call x1, Pallas kernels: 79.9 us -> 72.5 us  [block_step(): pl.pallas_call(kernel, out_shape=(pltpu.VMEM((ROWS, WIDTH), BF16), pltpu....]
where the time goes in v2:
time: 77.1 us; the launch traced here: 76.9 us
  Pallas kernels  76.1 us (99%)
  between operations  0.82 us (1%)
    pallas_call x1, Pallas kernels, block_step(): pl.pallas_call(kernel, out_shape=(pltpu.VMEM((ROWS, WIDTH), BF16), pltpu....  72.5 us
    pallas_call x1, Pallas kernels, block_step(): pl.pallas_call(writer, out_shape=(jax.ShapeDtypeStruct((ROWS, WIDTH), BF1...  3.62 us

profile of v2, /device:TPU:0, one launch (start us, length us, event | category | flops | bytes accessed | tf_op | source)
XLA Modules:
  0.0 76.9 jit_solution(16894922879646180504)
XLA Ops:
  0.6 72.5 %shard_map.126 = (bf16[2048,768]{1,0:T(8,128)(2,1)S(1)}, bf16[2048,768]{1,0:T(8,128)(2,1)S(1)}, f32[96,2304]{1,0:T(8,128)S(1)}, f32[96,768]{1,0:T(8,128)S(1)}, f...) custom-call(f32[16]{0:T(128)} %temp_ref.1, f32[768]{0:T(1024)} %gain_ref.1, f32[768]{0:T(1024)} %bias_ref.1, ...), custom_call_target="tpu_custom_call" | custom-call | tf_op jit(solution)/shard_map/pallas_call | solution.py:531
  73.1 3.6 %shard_map.127 = (bf16[2048,768]{1,0:T(8,128)(2,1)}, bf16[2048,768]{1,0:T(8,128)(2,1)}, f32[96,2304]{1,0:T(8,128)}, f32[96,768]{1,0:T(8,128)}, f32[768]{0:T(1024)}, /*index=5*/f32[768]{0:T(1024)}, f32[16]{0:T(128)}) custom-call(bf16[2048,768]{1,0:T(8,128)(2,1)S(1)} %get-tuple-element.13.out_v, bf16[2048,768]{1,0:T(8,128)(2,1)S(1)} %get-tuple-element.14.gtok_v, ...), custom_call_target="tpu_custom_call" | custom-call | tf_op jit(solution)/shard_map/pallas_call | solution.py:582

commit v3 on v2

--- a/solution.py
+++ b/solution.py
@@ -342,10 +342,10 @@
         for m in range(2):
             s1(ch, m).wait()
         s2_far(ch, 1 - cb)
+        s2_near(ch, 1 - cb)
         if not last:
             s2_far(ch, cb)
-        s2_near(ch, 1 - cb)
-        s2_near(ch, cb)
+            s2_near(ch, cb)
 
     def s3_copy(ch):
         return remote(r2.at[ch, 1 - cb], r3.at[ch], s3_send.at[ch], s3_recv.at[ch], second)
@@ -437,7 +437,7 @@
     ar(0, 0)
     for p in range(2):
         w_copy(1, p).wait()
-    loop(lambda b: project(2, block(b)), ((1, hook((0, 1))),))
+    loop(lambda b: project(2, block(b, BIG)), ((0, hook((0, 1))),), hi=ROWS // BIG)
     gram(1)
     ar(1, 0)
     for g in range(2):
@@ -491,8 +491,9 @@
     gw_chunks(6, 2)
     s3(3)
     last_step(0)
-    s2(6)
+    s2(6, True)
     s2(7, True)
+    s2_far(6, cb)
     s3(4)
     for b in range(1, NBLK + 1):
         last_step(b)
@@ -502,19 +503,22 @@
     for ch in range(4):
         s4(ch)
     gb_chips()
+    s3(7)
     s2_far(7, cb)
-    s4(4)
-    s3(7)
-    s4(5)
-    s4(6)
+    for ch in (6, 7):
+        s2_near(ch, cb)
+    for ch in (4, 5, 6):
+        s4(ch)
     gb_end()
     s4(7)
 
 
 def writer(out_v, gtok_v, gwq_v, gwo_v, gb_v, dtemp_v,
            out_hbm, gtok_hbm, gwq_hbm, gwo_hbm, gain_hbm, bias_hbm, dtemp_out, sem):
-    pairs = [(gtok_v, gtok_hbm), (out_v, out_hbm), (gwq_v, gwq_hbm), (gwo_v, gwo_hbm),
-             (gb_v.at[0], gain_hbm), (gb_v.at[1], bias_hbm)]
+    pairs = [(gb_v.at[0], gain_hbm), (gb_v.at[1], bias_hbm), (gwo_v, gwo_hbm), (gwq_v, gwq_hbm)]
+    for b in range(NBLK):
+        rows = pl.ds(b * BLK, BLK)
+        pairs += [(v.at[rows], hbm.at[rows]) for v, hbm in ((gtok_v, gtok_hbm), (out_v, out_hbm))]
     copies = [pltpu.make_async_copy(src, dst, sem.at[i]) for i, (src, dst) in enumerate(pairs)]
     for c in copies:
         c.start()
@@ -592,7 +596,7 @@
         ),
         in_specs=[vmem] * 6,
         out_specs=(hbm,) * 6 + (vmem,),
-        scratch_shapes=[dma((6,))],
+        scratch_shapes=[dma((4 + 2 * NBLK,))],
         compiler_params=pltpu.CompilerParams(vmem_limit_bytes=1000000),
     )(out, gtok, gwq, gwo, gb, dtemp)
 

time: 77.1 us -> 76.5 us (level)
  no operation moved by 1% of the time
where the time goes in v3:
time: 76.5 us; the launch traced here: 76.3 us
  Pallas kernels  75.5 us (99%)
  between operations  0.82 us (1%)
    pallas_call x1, Pallas kernels, block_step(): pl.pallas_call(kernel, out_shape=(pltpu.VMEM((ROWS, WIDTH), BF16), pltpu....  71.9 us
    pallas_call x1, Pallas kernels, block_step(): pl.pallas_call(writer, out_shape=(jax.ShapeDtypeStruct((ROWS, WIDTH), BF1...  3.64 us

profile of v3, /device:TPU:0, one launch (start us, length us, event | category | flops | bytes accessed | tf_op | source)
XLA Modules:
  0.0 76.3 jit_solution(13594691109890933997)
XLA Ops:
  0.6 71.9 %shard_map.126 = (bf16[2048,768]{1,0:T(8,128)(2,1)S(1)}, bf16[2048,768]{1,0:T(8,128)(2,1)S(1)}, f32[96,2304]{1,0:T(8,128)S(1)}, f32[96,768]{1,0:T(8,128)S(1)}, f...) custom-call(f32[16]{0:T(128)} %temp_ref.1, f32[768]{0:T(1024)} %gain_ref.1, f32[768]{0:T(1024)} %bias_ref.1, ...), custom_call_target="tpu_custom_call" | custom-call | tf_op jit(solution)/shard_map/pallas_call | solution.py:535
  72.5 3.6 %shard_map.127 = (bf16[2048,768]{1,0:T(8,128)(2,1)}, bf16[2048,768]{1,0:T(8,128)(2,1)}, f32[96,2304]{1,0:T(8,128)}, f32[96,768]{1,0:T(8,128)}, f32[768]{0:T(1024)}, /*index=5*/f32[768]{0:T(1024)}, f32[16]{0:T(128)}) custom-call(bf16[2048,768]{1,0:T(8,128)(2,1)S(1)} %get-tuple-element.13.out_v, bf16[2048,768]{1,0:T(8,128)(2,1)S(1)} %get-tuple-element.14.gtok_v, ...), custom_call_target="tpu_custom_call" | custom-call | tf_op jit(solution)/shard_map/pallas_call | solution.py:586

commit v4 on v3

--- a/solution.py
+++ b/solution.py
@@ -20,7 +20,7 @@
 BIG = 1024
 FINE = 256
 NFINE = ROWS // FINE
-LNR = 32
+LNR = 16
 PAIR = 192
 TOT = 2304
 LANES = 128

time: 76.5 us -> 76.3 us (level)
  no operation moved by 1% of the time
where the time goes in v4:
time: 76.3 us; the launch traced here: 76.2 us
  Pallas kernels  75.4 us (99%)
  between operations  0.82 us (1%)
    pallas_call x1, Pallas kernels, block_step(): pl.pallas_call(kernel, out_shape=(pltpu.VMEM((ROWS, WIDTH), BF16), pltpu....  71.7 us
    pallas_call x1, Pallas kernels, block_step(): pl.pallas_call(writer, out_shape=(jax.ShapeDtypeStruct((ROWS, WIDTH), BF1...  3.64 us

profile of v4, /device:TPU:0, one launch (start us, length us, event | category | flops | bytes accessed | tf_op | source)
XLA Modules:
  0.0 76.2 jit_solution(10732638774590438429)
XLA Ops:
  0.6 71.7 %shard_map.126 = (bf16[2048,768]{1,0:T(8,128)(2,1)S(1)}, bf16[2048,768]{1,0:T(8,128)(2,1)S(1)}, f32[96,2304]{1,0:T(8,128)S(1)}, f32[96,768]{1,0:T(8,128)S(1)}, f...) custom-call(f32[16]{0:T(128)} %temp_ref.1, f32[768]{0:T(1024)} %gain_ref.1, f32[768]{0:T(1024)} %bias_ref.1, ...), custom_call_target="tpu_custom_call" | custom-call | tf_op jit(solution)/shard_map/pallas_call | solution.py:535
  72.4 3.6 %shard_map.127 = (bf16[2048,768]{1,0:T(8,128)(2,1)}, bf16[2048,768]{1,0:T(8,128)(2,1)}, f32[96,2304]{1,0:T(8,128)}, f32[96,768]{1,0:T(8,128)}, f32[768]{0:T(1024)}, /*index=5*/f32[768]{0:T(1024)}, f32[16]{0:T(128)}) custom-call(bf16[2048,768]{1,0:T(8,128)(2,1)S(1)} %get-tuple-element.13.out_v, bf16[2048,768]{1,0:T(8,128)(2,1)S(1)} %get-tuple-element.14.gtok_v, ...), custom_call_target="tpu_custom_call" | custom-call | tf_op jit(solution)/shard_map/pallas_call | solution.py:586
